TPU v7x, 32 devices: a whole 2x2x4 slice. The times are simulated.
32 devices in a mesh: dp: 8 (over z, x), mp: 4 (over y, core).
Axes of the slice: x: 2, y: 2, z: 4, core: 2. Of those that a mesh axis runs over, the one named last changes fastest.
Arguments:
- tokens: bfloat16 [16384, 1024], P('dp'), may hold values from -6 to 6
- cotangent: bfloat16 [16384, 1024], P('dp'), may hold values from -15 to 15
- item_lengths: int32 [8, 8], P('dp'), may hold values from 1 to 1024, 2048 in all within a row
- w_qkv: bfloat16 [3, 1024, 1024], P(None, None, 'mp'), may hold values from -0.1875 to 0.1875
- b_qv: float32 [2, 1024], P(None, 'mp'), may hold values from -3 to 3
- w_out: bfloat16 [1024, 1024], P('mp'), may hold values from -0.75 to 0.75
- b_out: float32 [1024], replicated, may hold values from -1.75 to 1.75
- w_fc1: bfloat16 [1024, 4096], P(None, 'mp'), may hold values from -0.1875 to 0.1875
- b_fc1: float32 [4096], P('mp'), may hold values from -3 to 3
- w_fc2: bfloat16 [4096, 1024], P('mp'), may hold values from -0.09375 to 0.09375
- b_fc2: float32 [1024], replicated, may hold values from -1.75 to 1.75
- ln1_gain: float32 [1024], replicated, may hold values from 0.5 to 1.5
- ln1_bias: float32 [1024], replicated, may hold values from -1.75 to 1.75
- ln2_gain: float32 [1024], replicated, may hold values from 0.5 to 1.5
- ln2_bias: float32 [1024], replicated, may hold values from -1.75 to 1.75
Outputs:
- output: bfloat16 [16384, 1024], P('dp')
- grad_tokens: float32 [16384, 1024], P('dp')
- grad_w_qkv: float32 [3, 1024, 1024], P(None, 'dp', 'mp')
- grad_b_qv: float32 [2, 1024], P(None, 'mp')
- grad_w_out: float32 [1024, 1024], P('mp', 'dp')
- grad_b_out: float32 [1024], replicated
- grad_w_fc1: float32 [1024, 4096], P('dp', 'mp')
- grad_b_fc1: float32 [4096], P('mp')
- grad_w_fc2: float32 [4096, 1024], P('mp', 'dp')
- grad_b_fc2: float32 [1024], replicated
- grad_ln1_gain: float32 [1024], replicated
- grad_ln1_bias: float32 [1024], replicated
- grad_ln2_gain: float32 [1024], replicated
- grad_ln2_bias: float32 [1024], replicated
Inputs may be any that keep to these rules, and one draw needn't show every extreme that they name: `item_lengths`: each row sums to 2048, and each row's longest item has exactly 1024 patches.
All inputs are finite; a program needn't handle non-finite values.
Results may differ from a plain program's by a relative error of at most 0.019.
Values may be sent and summed in bfloat16 or wider, within the bound.
A program may use at most 192 MiB of HBM per device.

v0:
```python
import jax
import jax.numpy as jnp
from jax import lax
from jax.sharding import PartitionSpec as P

HEAD = 64
QBLOCK = 512


def normalize(values, gain, shift):
    center = jnp.mean(values, axis=-1, keepdims=True)
    centered = values - center
    spread = jnp.mean(centered * centered, axis=-1, keepdims=True)
    return centered * lax.rsqrt(spread + 1e-06) * gain + shift


def exact_gelu(values):
    return jax.nn.gelu(values, approximate=False)


def segment_ids(lengths_row, row_count):
    ends = jnp.cumsum(lengths_row)
    positions = jnp.arange(row_count, dtype=jnp.int32)
    return jnp.sum((positions[:, None] >= ends[None, :]).astype(jnp.int32), axis=1)


def per_device(
    tokens,
    cotangent,
    item_lengths,
    w_qkv,
    b_qv,
    w_out,
    b_out,
    w_fc1,
    b_fc1,
    w_fc2,
    b_fc2,
    ln1_gain,
    ln1_bias,
    ln2_gain,
    ln2_bias,
):
    row_count = tokens.shape[0]
    local_cols = w_qkv.shape[2]
    heads_here = local_cols // HEAD
    blocks = row_count // QBLOCK
    score_scale = HEAD ** (-0.5)
    segments = segment_ids(item_lengths[0], row_count)
    seg_blocks = segments.reshape(blocks, QBLOCK)
    inputs = tokens.astype(jnp.float32)
    norm_one, norm_one_back = jax.vjp(normalize, inputs, ln1_gain, ln1_bias)
    normed_one = norm_one.astype(jnp.bfloat16)
    queries = (jnp.dot(normed_one, w_qkv[0], preferred_element_type=jnp.float32) + b_qv[0]).astype(
        jnp.bfloat16
    )
    key_rows = jnp.dot(normed_one, w_qkv[1], preferred_element_type=jnp.float32).astype(
        jnp.bfloat16
    )
    value_rows = (
        jnp.dot(normed_one, w_qkv[2], preferred_element_type=jnp.float32) + b_qv[1]
    ).astype(jnp.bfloat16)
    key_heads = key_rows.reshape(row_count, heads_here, HEAD)
    value_heads = value_rows.reshape(row_count, heads_here, HEAD)
    query_blocks = queries.reshape(blocks, QBLOCK, heads_here, HEAD)

    def block_scores(query_block, seg_block):
        scores = (
            jnp.einsum("qhd,khd->hqk", query_block, key_heads, preferred_element_type=jnp.float32)
            * score_scale
        )
        same = seg_block[:, None] == segments[None, :]
        return jnp.where(same[None], scores, -1e30)

    def forward_block(pieces):
        query_block, seg_block = pieces
        scores = block_scores(query_block, seg_block)
        row_max = jnp.max(scores, axis=-1, keepdims=True)
        raised = jnp.exp(scores - row_max)
        row_sum = jnp.sum(raised, axis=-1, keepdims=True)
        probs = raised / row_sum
        block_out = jnp.einsum(
            "hqk,khd->qhd",
            probs.astype(jnp.bfloat16),
            value_heads,
            preferred_element_type=jnp.float32,
        )
        return (block_out.astype(jnp.bfloat16), (row_max + jnp.log(row_sum))[..., 0])

    out_blocks, log_norms = lax.map(forward_block, (query_blocks, seg_blocks))
    attended = out_blocks.reshape(row_count, local_cols)
    attention_sum = lax.psum(
        jnp.dot(attended, w_out, preferred_element_type=jnp.float32).astype(jnp.bfloat16), "mp"
    ).astype(jnp.float32)
    middle = inputs + attention_sum + b_out
    norm_two, norm_two_back = jax.vjp(normalize, middle, ln2_gain, ln2_bias)
    normed_two = norm_two.astype(jnp.bfloat16)
    hidden_pre = jnp.dot(normed_two, w_fc1, preferred_element_type=jnp.float32) + b_fc1
    activated_full, gelu_back = jax.vjp(exact_gelu, hidden_pre)
    activated = activated_full.astype(jnp.bfloat16)
    mlp_sum = lax.psum(
        jnp.dot(activated, w_fc2, preferred_element_type=jnp.float32).astype(jnp.bfloat16), "mp"
    ).astype(jnp.float32)
    output = (middle + mlp_sum + b_fc2).astype(jnp.bfloat16)
    upstream = cotangent.astype(jnp.float32)
    grad_b_fc2 = jnp.sum(upstream, axis=0)
    grad_w_fc2 = jnp.einsum("tf,td->fd", activated, cotangent, preferred_element_type=jnp.float32)
    d_act = jnp.einsum("td,fd->tf", cotangent, w_fc2, preferred_element_type=jnp.float32)
    d_pre = gelu_back(d_act)[0]
    grad_b_fc1 = jnp.sum(d_pre, axis=0)
    d_pre_low = d_pre.astype(jnp.bfloat16)
    grad_w_fc1 = jnp.einsum("td,tf->df", normed_two, d_pre_low, preferred_element_type=jnp.float32)
    d_normed_two = lax.psum(
        jnp.einsum("tf,df->td", d_pre_low, w_fc1, preferred_element_type=jnp.float32).astype(
            jnp.bfloat16
        ),
        "mp",
    ).astype(jnp.float32)
    d_middle_norm, grad_ln2_gain, grad_ln2_bias = norm_two_back(d_normed_two)
    d_middle = upstream + d_middle_norm
    grad_b_out = jnp.sum(d_middle, axis=0)
    d_middle_low = d_middle.astype(jnp.bfloat16)
    grad_w_out = jnp.einsum("tc,td->cd", attended, d_middle_low, preferred_element_type=jnp.float32)
    d_attended = jnp.einsum(
        "td,cd->tc", d_middle_low, w_out, preferred_element_type=jnp.float32
    ).astype(jnp.bfloat16)
    d_att_blocks = d_attended.reshape(blocks, QBLOCK, heads_here, HEAD)

    def backward_block(running, pieces):
        d_keys_acc, d_values_acc = running
        query_block, seg_block, d_out_block, log_norm = pieces
        scores = block_scores(query_block, seg_block)
        probs = jnp.exp(scores - log_norm[..., None])
        d_probs = jnp.einsum(
            "qhd,khd->hqk", d_out_block, value_heads, preferred_element_type=jnp.float32
        )
        d_scores = probs * (d_probs - jnp.sum(probs * d_probs, axis=-1, keepdims=True))
        d_scores_low = d_scores.astype(jnp.bfloat16)
        d_query_block = (
            jnp.einsum("hqk,khd->qhd", d_scores_low, key_heads, preferred_element_type=jnp.float32)
            * score_scale
        )
        d_keys_acc = (
            d_keys_acc
            + jnp.einsum(
                "hqk,qhd->khd", d_scores_low, query_block, preferred_element_type=jnp.float32
            )
            * score_scale
        )
        d_values_acc = d_values_acc + jnp.einsum(
            "hqk,qhd->khd",
            probs.astype(jnp.bfloat16),
            d_out_block,
            preferred_element_type=jnp.float32,
        )
        return ((d_keys_acc, d_values_acc), d_query_block)

    zeros_acc = jnp.zeros((row_count, heads_here, HEAD), jnp.float32)
    (d_keys, d_values), d_query_blocks = lax.scan(
        backward_block, (zeros_acc, zeros_acc), (query_blocks, seg_blocks, d_att_blocks, log_norms)
    )
    d_queries = d_query_blocks.reshape(row_count, local_cols)
    d_keys = d_keys.reshape(row_count, local_cols)
    d_values = d_values.reshape(row_count, local_cols)
    grad_b_qv = jnp.stack([jnp.sum(d_queries, axis=0), jnp.sum(d_values, axis=0)])
    stacked = jnp.stack([d_queries, d_keys, d_values]).astype(jnp.bfloat16)
    grad_w_qkv = jnp.einsum("td,stc->sdc", normed_one, stacked, preferred_element_type=jnp.float32)
    d_normed_one = lax.psum(
        jnp.einsum("stc,sdc->td", stacked, w_qkv, preferred_element_type=jnp.float32).astype(
            jnp.bfloat16
        ),
        "mp",
    ).astype(jnp.float32)
    d_input_norm, grad_ln1_gain, grad_ln1_bias = norm_one_back(d_normed_one)
    grad_tokens = d_middle + d_input_norm
    summed_qkv, summed_out, summed_fc1, summed_fc2 = (
        lax.psum_scatter(grad_w_qkv, "dp", scatter_dimension=1, tiled=True),
        lax.psum_scatter(grad_w_out, "dp", scatter_dimension=1, tiled=True),
        lax.psum_scatter(grad_w_fc1, "dp", scatter_dimension=0, tiled=True),
        lax.psum_scatter(grad_w_fc2, "dp", scatter_dimension=1, tiled=True),
    )
    small_sums = lax.psum(
        (
            grad_ln1_gain,
            grad_ln1_bias,
            grad_ln2_gain,
            grad_ln2_bias,
            grad_b_out,
            grad_b_fc2,
            grad_b_qv,
            grad_b_fc1,
        ),
        "dp",
    )
    return (
        output,
        grad_tokens,
        summed_qkv,
        small_sums[6],
        summed_out,
        small_sums[4],
        summed_fc1,
        small_sums[7],
        summed_fc2,
        small_sums[5],
        small_sums[0],
        small_sums[1],
        small_sums[2],
        small_sums[3],
    )


def solution(mesh):
    in_specs = (
        P("dp", None),
        P("dp", None),
        P("dp", None),
        P(None, None, "mp"),
        P(None, "mp"),
        P("mp", None),
        P(),
        P(None, "mp"),
        P("mp"),
        P("mp", None),
        P(),
        P(),
        P(),
        P(),
        P(),
    )
    out_specs = (
        P("dp", None),
        P("dp", None),
        P(None, "dp", "mp"),
        P(None, "mp"),
        P("mp", "dp"),
        P(),
        P("dp", "mp"),
        P("mp"),
        P("mp", "dp"),
        P(),
        P(),
        P(),
        P(),
        P(),
    )
    return jax.shard_map(
        per_device, mesh=mesh, in_specs=in_specs, out_specs=out_specs, check_vma=False
    )
```

profile of v0, /device:TPU:0, one launch (start us, length us, event | category | flops | bytes accessed | tf_op | source)
XLA Modules:
  0.0 1066.7 jit_solution(14940275114370547031)
XLA Ops:
  32.3 64.4 %while.27 = (s32[]{:T(128)}, bf16[4,512,4,64]{1,3,2,0:T(8,128)(2,1)}, f32[4,4,512]{2,1,0:T(4,128)}, s32[4,512]{1,0:T(4,128)S(1)}, s32[2048]{0:T(1024)S(1)}, /*in...) while((s32[]{:T(128)}, ...), condition=%wide.region_7.8_spmd, body=%wide.region_4.7_spmd.sunk | while | flops 1125251072 | bytes 61421712 | solution.py:90
  41.8 5.9 fusion.148
  57.8 5.9 fusion.148
  73.8 5.9 fusion.148
  89.8 5.9 fusion.148
  105.5 88.3 %all-reduce.6.cloned.1.call-done = bf16[2048,1024]{1,0:T(8,128)(2,1)} async-done(((bf16[2048,1024]{1,0:T(8,128)(2,1)}), bf16[2048,1024]{1,0:T(8,128)(2,1)}) %all-reduce.6.cloned.1.call-update) | async-done | bytes 4194320 | tf_op jit(solution)/shard_map/psum | solution.py:92
  201.9 5.8 fusion.91
  207.7 25.4 %fusion.94 = (f32[1024]{0:T(1024)}, bf16[2048,1024]{1,0:T(8,128)(2,1)S(1)}, f32[2048,1024]{1,0:T(8,128)}) fusion(f32[2048,1024]{1,0:T(8,128)S(1)} %fusion.91, f32[1024]{0:T(1024)S(1)} %copy-done.52, bf16[2048,1024]{1,0:T(8,128)(2,1)S(1)} %copy-done.21, bf16[1024,1024]{1,0:T(8,128)(2,1)S(1)} %copy-done), kind=kOutput, calls=%fused_computation.147 | convolution fusion | flops 4450155520 | bytes 27271168 | tf_op jit(solution)/shard_map/td,fd->tf/dot_general | solution.py:108
  235.1 6.3 convolution_convert_fusion.1
  241.7 10.4 multiply_convert_fusion.1
  252.1 8.4 convolution_convert_fusion.2
  260.5 66.8 %all-reduce.8.cloned.1.call-done = bf16[2048,1024]{1,0:T(8,128)(2,1)} async-done(((bf16[2048,1024]{1,0:T(8,128)(2,1)}), bf16[2048,1024]{1,0:T(8,128)(2,1)}) %all-reduce.8.cloned.1.call-update) | async-done | bytes 4194320 | tf_op jit(solution)/shard_map/psum | solution.py:113
  327.3 8.5 convert_reduce_fusion.1
  335.8 7.0 fusion.57
  342.8 6.3 fusion.96
  360.5 195.5 %while.28 = (s32[]{:T(128)}, f32[2048,4,64]{0,2,1:T(8,128)}, f32[2048,4,64]{0,2,1:T(8,128)}, f32[4,512,4,64]{1,3,2,0:T(8,128)}, bf16[4,512,4,64]{1,3,2,0:T(8,128...) while((s32[]{:T(128)}, f32[2048,4,64]{0,2,1:T(8,128)}, ...), condition=%wide.region_17.18_spmd.clone, body=%wide.region_15.17_spmd.clone.sunk | while | flops 2751068160 | bytes 164206880 | solution.py:159
  366.5 7.2 fusion.160
  373.7 11.5 %multiply_reduce_fusion.3 = (f32[4,512]{1,0:T(4,128)}, f32[4,512,2048]{2,1,0:T(8,128)}) fusion(f32[4,512,2048]{2,1,0:T(8,128)S(1)} %fusion.158, f32[4,512]{1,0:T(4,128)S(1)} %dynamic-slice_bitcast_fusion.2, pred[512,2048]{1,0:T(8,128)(4,1)} %copy-done.8, bf16[2048,4,64]{0,2,1:T(8,128)(2,1)} %get-tuple-element.520, ...), kind=kOutput, calls=%fused_computation.19.clone.1 | convolution fusion | flops 557840384 | bytes 35930116 | tf_op jit(solution)/shard_map/while/body/eval_jaxpr/qhd,khd->hqk/dot_general | solution.py:134
  385.2 11.1 %multiply_convert_fusion.3 = bf16[4,512,2048]{2,1,0:T(8,128)(2,1)} fusion(f32[4,512,2048]{2,1,0:T(8,128)} %get-tuple-element.455, f32[4,512,2048]{2,1,0:T(8,128)S(1)} %fusion.158, f32[4,512]{1,0:T(4,128)} %get-tuple-element.456, f32[4,512]{1,0:T(4,128)S(1)} %dynamic-slice_bitcast_fusion.2, pred[512,2048]{1,0:T(8,128)(4,1)} %copy-done.8), kind=kLoop, calls=%fused_computation.18.clone.1 | loop fusion | flops 25165824 | bytes 43008000 | tf_op jit(solution)/shard_map/while/body/eval_jaxpr/convert_element_type | solution.py:138
  396.3 5.3 fusion.159
  401.6 7.7 fusion.161
  414.9 7.6 fusion.160
  422.5 11.5 %multiply_reduce_fusion.3 = (f32[4,512]{1,0:T(4,128)}, f32[4,512,2048]{2,1,0:T(8,128)}) fusion(f32[4,512,2048]{2,1,0:T(8,128)S(1)} %fusion.158, f32[4,512]{1,0:T(4,128)S(1)} %dynamic-slice_bitcast_fusion.2, pred[512,2048]{1,0:T(8,128)(4,1)} %copy-done.8, bf16[2048,4,64]{0,2,1:T(8,128)(2,1)} %get-tuple-element.520, ...), kind=kOutput, calls=%fused_computation.19.clone.1 | convolution fusion | flops 557840384 | bytes 35930116 | tf_op jit(solution)/shard_map/while/body/eval_jaxpr/qhd,khd->hqk/dot_general | solution.py:134
  434.0 11.1 %multiply_convert_fusion.3 = bf16[4,512,2048]{2,1,0:T(8,128)(2,1)} fusion(f32[4,512,2048]{2,1,0:T(8,128)} %get-tuple-element.455, f32[4,512,2048]{2,1,0:T(8,128)S(1)} %fusion.158, f32[4,512]{1,0:T(4,128)} %get-tuple-element.456, f32[4,512]{1,0:T(4,128)S(1)} %dynamic-slice_bitcast_fusion.2, pred[512,2048]{1,0:T(8,128)(4,1)} %copy-done.8), kind=kLoop, calls=%fused_computation.18.clone.1 | loop fusion | flops 25165824 | bytes 43008000 | tf_op jit(solution)/shard_map/while/body/eval_jaxpr/convert_element_type | solution.py:138
  445.1 5.3 fusion.159
  450.5 7.7 fusion.161
  463.7 7.6 fusion.160
  471.4 11.5 %multiply_reduce_fusion.3 = (f32[4,512]{1,0:T(4,128)}, f32[4,512,2048]{2,1,0:T(8,128)}) fusion(f32[4,512,2048]{2,1,0:T(8,128)S(1)} %fusion.158, f32[4,512]{1,0:T(4,128)S(1)} %dynamic-slice_bitcast_fusion.2, pred[512,2048]{1,0:T(8,128)(4,1)} %copy-done.8, bf16[2048,4,64]{0,2,1:T(8,128)(2,1)} %get-tuple-element.520, ...), kind=kOutput, calls=%fused_computation.19.clone.1 | convolution fusion | flops 557840384 | bytes 35930116 | tf_op jit(solution)/shard_map/while/body/eval_jaxpr/qhd,khd->hqk/dot_general | solution.py:134
  482.9 11.1 %multiply_convert_fusion.3 = bf16[4,512,2048]{2,1,0:T(8,128)(2,1)} fusion(f32[4,512,2048]{2,1,0:T(8,128)} %get-tuple-element.455, f32[4,512,2048]{2,1,0:T(8,128)S(1)} %fusion.158, f32[4,512]{1,0:T(4,128)} %get-tuple-element.456, f32[4,512]{1,0:T(4,128)S(1)} %dynamic-slice_bitcast_fusion.2, pred[512,2048]{1,0:T(8,128)(4,1)} %copy-done.8), kind=kLoop, calls=%fused_computation.18.clone.1 | loop fusion | flops 25165824 | bytes 43008000 | tf_op jit(solution)/shard_map/while/body/eval_jaxpr/convert_element_type | solution.py:138
  499.3 7.7 fusion.161
  512.6 7.6 fusion.160
  520.2 11.5 %multiply_reduce_fusion.3 = (f32[4,512]{1,0:T(4,128)}, f32[4,512,2048]{2,1,0:T(8,128)}) fusion(f32[4,512,2048]{2,1,0:T(8,128)S(1)} %fusion.158, f32[4,512]{1,0:T(4,128)S(1)} %dynamic-slice_bitcast_fusion.2, pred[512,2048]{1,0:T(8,128)(4,1)} %copy-done.8, bf16[2048,4,64]{0,2,1:T(8,128)(2,1)} %get-tuple-element.520, ...), kind=kOutput, calls=%fused_computation.19.clone.1 | convolution fusion | flops 557840384 | bytes 35930116 | tf_op jit(solution)/shard_map/while/body/eval_jaxpr/qhd,khd->hqk/dot_general | solution.py:134
  531.7 11.1 %multiply_convert_fusion.3 = bf16[4,512,2048]{2,1,0:T(8,128)(2,1)} fusion(f32[4,512,2048]{2,1,0:T(8,128)} %get-tuple-element.455, f32[4,512,2048]{2,1,0:T(8,128)S(1)} %fusion.158, f32[4,512]{1,0:T(4,128)} %get-tuple-element.456, f32[4,512]{1,0:T(4,128)S(1)} %dynamic-slice_bitcast_fusion.2, pred[512,2048]{1,0:T(8,128)(4,1)} %copy-done.8), kind=kLoop, calls=%fused_computation.18.clone.1 | loop fusion | flops 25165824 | bytes 43008000 | tf_op jit(solution)/shard_map/while/body/eval_jaxpr/convert_element_type | solution.py:138
  548.1 7.6 fusion.161
  568.1 7.5 bitcast_convert_fusion
  576.8 7.7 fusion.77
  584.6 5.6 fusion.71
  590.3 10.0 fusion.100
  600.7 12.4 %fusion.74 = f32[1024,1024]{1,0:T(8,128)} fusion(bf16[2048,1024]{1,0:T(8,128)(2,1)} %copy-done.57, f32[1024]{0:T(1024)S(1)} %copy-done.56, f32[1024]{0:T(1024)S(1)} %copy-done.44, f32[2048]{0:T(1024)S(1)} %copy-done.38, bf16[2048,1024]{1,0:T(8,128)(2,1)} %all-reduce.6.cloned.1.call-done, bf16[2048,1024]{1,0:T(8,128)(2,1)} %param.19, ...), kind=kOutput, calls=%fused_computation.120 | convolution fusion | flops 4313841664 | bytes 16805888 | tf_op jit(solution)/shard_map/td,tf->df/dot_general | solution.py:112
  613.3 115.5 %all-reduce.10.cloned.1.call-done = (bf16[2048,1024]{1,0:T(8,128)(2,1)}, bf16[2048,1024]{1,0:T(8,128)(2,1)}) async-done(((bf16[2048,1024]{1,0:T(8,128)(2,1)}, bf16[2048,1024]{1,0:T(8,128)(2,1)}), (bf16[2048,1024]{1,0:T(8,128)(2,1)}, bf16[2048,1024]{1,0:T(8,128)(2,1)})) %all-reduce.10.cloned.1.call-update) | async-done | bytes 8388624 | tf_op jit(solution)/shard_map/psum | solution.py:101
  728.9 5.7 convert_reduce_fusion
  734.7 5.4 fusion.58
  740.2 38.7 %all-reduce = (f32[2,256]{1,0:T(2,128)}, f32[1024]{0:T(1024)}, f32[1024]{0:T(1024)}, f32[1024]{0:T(1024)}, f32[1024]{0:T(1024)}, /*index=5*/f32[1024]{0:T(1024)}, f32[1024]{0:T(1024)}, f32[1024]{0:T(1024)}) all-reduce(f32[2,256]{1,0:T(2,128)S(1)} %pad_maximum_fusion.3, ...), channel_id=1, replica_groups=mesh['dp'=8,'mp'=4] {'dp'}, use_global_device_ids=true, to_apply=%region_24.25 | all-reduce | flops 7680 | bytes 61440 | tf_op jit(solution)/shard_map/psum | solution.py:182
  778.9 16.0 %add_add_fusion.2 = (f32[2048,1024]{1,0:T(8,128)}, bf16[2048,1024]{1,0:T(8,128)(2,1)}) fusion(f32[2048,1024]{1,0:T(8,128)} %copy-done.9, bf16[2048,1024]{1,0:T(8,128)(2,1)} %param.19, bf16[2048,1024]{1,0:T(8,128)(2,1)} %get-tuple-element.311, f32[2048]{0:T(1024)S(1)} %negate_multiply_fusion.1, f32[2048]{0:T(1024)S(1)} %multiply_multiply_fusion.5, ...), kind=kLoop, calls=%fused_computation.83 | loop fusion | flops 35651584 | bytes 37793792 | tf_op jit(solution)/shard_map/add | solution.py:175
  794.9 13.0 %reduce-scatter.5.cloned.1.call-done = f32[3,128,256]{1,2,0:T(8,128)} async-done(((f32[3,1024,256]{1,2,0:T(8,128)}), f32[3,128,256]{1,2,0:T(8,128)}) %reduce-scatter.5.cloned.1.call-update) | async-done | bytes 393232 | tf_op jit(solution)/shard_map/reduce_scatter | solution.py:177
  809.8 65.8 %reduce-scatter.7.cloned.1.call-done = f32[256,128]{1,0:T(8,128)} async-done(((f32[256,1024]{1,0:T(8,128)}), f32[256,128]{1,0:T(8,128)}) %reduce-scatter.7.cloned.1.call-update) | async-done | bytes 131088 | tf_op jit(solution)/shard_map/reduce_scatter | solution.py:178
  875.6 91.7 %reduce-scatter.11.cloned.1.call-done = f32[1024,128]{1,0:T(8,128)} async-done(((f32[1024,1024]{1,0:T(8,128)}), f32[1024,128]{1,0:T(8,128)}) %reduce-scatter.11.cloned.1.call-update) | async-done | bytes 524304 | tf_op jit(solution)/shard_map/reduce_scatter | solution.py:180
  967.3 92.2 %reduce-scatter.9.cloned.1.call-done = f32[128,1024]{1,0:T(8,128)} async-done(((f32[1024,1024]{1,0:T(8,128)}), f32[128,1024]{1,0:T(8,128)}) %reduce-scatter.9.cloned.1.call-update) | async-done | bytes 524304 | tf_op jit(solution)/shard_map/reduce_scatter | solution.py:179
  (242 shorter events, 144.5 us)
Async XLA Ops:
  7.2 200.5 %copy-start = (bf16[1024,1024]{1,0:T(8,128)(2,1)S(1)}, bf16[1024,1024]{1,0:T(8,128)(2,1)}, u32[]{:S(2)}) copy-start(bf16[1024,1024]{1,0:T(8,128)(2,1)} %param.28) | copy-start | bytes 6291460
  7.2 9.1 copy-start.41
  7.2 9.1 copy-start.49
  7.2 186.6 %all-reduce.6.cloned.1.call-start = ((), (), s32[]{:S(2)}) async-start(), calls=%async_computation.4 | async-start | bytes 8388608 | tf_op jit(solution)/shard_map/psum | solution.py:92
  9.1 8.9 copy-start.54
  97.3 8.1 copy-start.6
  97.3 8.1 copy-start.24
  97.3 96.4 %copy-start.32 = (f32[1024]{0:T(1024)S(1)}, f32[1024]{0:T(1024)}, u32[]{:S(2)}) copy-start(f32[1024]{0:T(1024)} %param.25) | copy-start | bytes 12292
  105.4 96.4 %copy-start.43 = (f32[1024]{0:T(1024)S(1)}, f32[1024]{0:T(1024)}, u32[]{:S(2)}) copy-start(f32[1024]{0:T(1024)} %param.32) | copy-start | bytes 12292
  105.4 96.4 %copy-start.55 = (f32[1024]{0:T(1024)S(1)}, f32[1024]{0:T(1024)}, u32[]{:S(2)}) copy-start(f32[1024]{0:T(1024)} %param.33) | copy-start | bytes 12292
  105.5 221.8 %all-reduce.8.cloned.1.call-start = ((), (), s32[]{:S(2)}) async-start(), calls=%async_computation.5 | async-start | bytes 8388608 | tf_op jit(solution)/shard_map/psum | solution.py:113
  199.7 143.1 %copy-start.30 = (f32[2048]{0:T(1024)}, f32[2048]{0:T(1024)S(1)}, u32[]{:S(2)}) copy-start(f32[2048]{0:T(1024)S(1)} %broadcast_multiply_fusion) | copy-start | bytes 24580
  201.8 140.9 %copy-start.37 = (f32[2048]{0:T(1024)}, f32[2048]{0:T(1024)S(1)}, u32[]{:S(2)}) copy-start(f32[2048]{0:T(1024)S(1)} %fusion.87) | copy-start | bytes 24580
  207.7 25.4 %copy-start.19 = (f32[2048,1024]{1,0:T(8,128)}, f32[2048,1024]{1,0:T(8,128)S(1)}, u32[]{:S(2)}) copy-start(f32[2048,1024]{1,0:T(8,128)S(1)} %fusion.91) | copy-start | bytes 25165828
  241.5 487.3 %all-reduce.10.cloned.1.call-start = ((), (), s32[]{:S(2)}) async-start(), calls=%async_computation.10 | async-start | bytes 16777216 | tf_op jit(solution)/shard_map/psum | solution.py:101
  327.2 8.5 copy-start.4
  327.2 8.5 copy-start.11
  327.3 8.5 copy-start.15
  342.8 9.8 copy-start.23
  385.2 11.1 %copy-start.12 = (f32[2048,4,64]{0,2,1:T(8,128)S(1)}, f32[2048,4,64]{0,2,1:T(8,128)}, u32[]{:S(2)}) copy-start(f32[2048,4,64]{0,2,1:T(8,128)} %get-tuple-element.498) | copy-start | bytes 6291460 | tf_op jit(solution)/shard_map/while
  396.3 13.0 %copy-start.26 = (s32[2048]{0:T(1024)S(1)}, s32[2048]{0:T(1024)}, u32[]{:S(2)}) copy-start(s32[2048]{0:T(1024)} %get-tuple-element.570) | copy-start | bytes 24580 | tf_op jit(solution)/shard_map/while
  434.0 11.1 %copy-start.12 = (f32[2048,4,64]{0,2,1:T(8,128)S(1)}, f32[2048,4,64]{0,2,1:T(8,128)}, u32[]{:S(2)}) copy-start(f32[2048,4,64]{0,2,1:T(8,128)} %get-tuple-element.498) | copy-start | bytes 6291460 | tf_op jit(solution)/shard_map/while
  445.1 13.0 %copy-start.26 = (s32[2048]{0:T(1024)S(1)}, s32[2048]{0:T(1024)}, u32[]{:S(2)}) copy-start(s32[2048]{0:T(1024)} %get-tuple-element.570) | copy-start | bytes 24580 | tf_op jit(solution)/shard_map/while
  482.8 11.1 %copy-start.12 = (f32[2048,4,64]{0,2,1:T(8,128)S(1)}, f32[2048,4,64]{0,2,1:T(8,128)}, u32[]{:S(2)}) copy-start(f32[2048,4,64]{0,2,1:T(8,128)} %get-tuple-element.498) | copy-start | bytes 6291460 | tf_op jit(solution)/shard_map/while
  494.0 13.0 %copy-start.26 = (s32[2048]{0:T(1024)S(1)}, s32[2048]{0:T(1024)}, u32[]{:S(2)}) copy-start(s32[2048]{0:T(1024)} %get-tuple-element.570) | copy-start | bytes 24580 | tf_op jit(solution)/shard_map/while
  531.7 11.1 %copy-start.12 = (f32[2048,4,64]{0,2,1:T(8,128)S(1)}, f32[2048,4,64]{0,2,1:T(8,128)}, u32[]{:S(2)}) copy-start(f32[2048,4,64]{0,2,1:T(8,128)} %get-tuple-element.498) | copy-start | bytes 6291460 | tf_op jit(solution)/shard_map/while
  542.8 13.0 %copy-start.26 = (s32[2048]{0:T(1024)S(1)}, s32[2048]{0:T(1024)}, u32[]{:S(2)}) copy-start(s32[2048]{0:T(1024)} %get-tuple-element.570) | copy-start | bytes 24580 | tf_op jit(solution)/shard_map/while
  575.6 8.9 copy-start.18
  575.6 232.3 %reduce-scatter.5.cloned.1.call-start = ((), (), s32[]{:S(2)}) async-start(), calls=%async_computation.6 | async-start | bytes 3538944 | tf_op jit(solution)/shard_map/reduce_scatter | solution.py:177
  584.5 291.1 %reduce-scatter.7.cloned.1.call-start = ((), (), s32[]{:S(2)}) async-start(), calls=%async_computation.7 | async-start | bytes 1179648 | tf_op jit(solution)/shard_map/reduce_scatter | solution.py:178
  590.2 10.4 copy-start.31
  590.2 10.4 copy-start.33
  590.2 10.4 copy-start.38
  590.2 10.4 copy-start.44
  590.2 10.4 copy-start.56
  590.3 377.0 %reduce-scatter.11.cloned.1.call-start = ((), (), s32[]{:S(2)}) async-start(), calls=%async_computation.9 | async-start | bytes 4718592 | tf_op jit(solution)/shard_map/reduce_scatter | solution.py:180
  600.3 128.5 %copy-start.29 = (f32[2048]{0:T(1024)S(1)}, f32[2048]{0:T(1024)}, u32[]{:S(2)}) copy-start(f32[2048]{0:T(1024)} %copy-done.28) | copy-start | bytes 24580
  600.4 128.5 %copy-start.42 = (f32[1024]{0:T(1024)S(1)}, f32[1024]{0:T(1024)}, u32[]{:S(2)}) copy-start(f32[1024]{0:T(1024)} %param.30) | copy-start | bytes 12292
  600.4 459.1 %reduce-scatter.9.cloned.1.call-start = ((), (), s32[]{:S(2)}) async-start(), calls=%async_computation.8 | async-start | bytes 4718592 | tf_op jit(solution)/shard_map/reduce_scatter | solution.py:179
  613.1 121.4 %copy-start.40 = (f32[2048]{0:T(1024)S(1)}, f32[2048]{0:T(1024)}, u32[]{:S(2)}) copy-start(f32[2048]{0:T(1024)} %copy-done.39) | copy-start | bytes 24580
  613.1 121.5 %copy-start.35 = (f32[2048]{0:T(1024)S(1)}, f32[2048]{0:T(1024)}, u32[]{:S(2)}) copy-start(f32[2048]{0:T(1024)} %copy-done.34) | copy-start | bytes 24580
  728.8 11.3 %copy-start.45 = (f32[1024]{0:T(1024)S(1)}, f32[1024]{0:T(1024)}, u32[]{:S(2)}) copy-start(f32[1024]{0:T(1024)} %get-tuple-element.260) | copy-start | bytes 12292
  728.8 11.3 %copy-start.46 = (f32[1024]{0:T(1024)S(1)}, f32[1024]{0:T(1024)}, u32[]{:S(2)}) copy-start(f32[1024]{0:T(1024)} %get-tuple-element.256) | copy-start | bytes 12292
  728.8 11.3 %copy-start.47 = (f32[1024]{0:T(1024)S(1)}, f32[1024]{0:T(1024)}, u32[]{:S(2)}) copy-start(f32[1024]{0:T(1024)} %get-tuple-element.315) | copy-start | bytes 12292
  728.8 11.3 %copy-start.48 = (f32[1024]{0:T(1024)S(1)}, f32[1024]{0:T(1024)}, u32[]{:S(2)}) copy-start(f32[1024]{0:T(1024)} %get-tuple-element.321) | copy-start | bytes 12292
  728.9 11.3 %copy-start.51 = (f32[1024]{0:T(1024)S(1)}, f32[1024]{0:T(1024)}, u32[]{:S(2)}) copy-start(f32[1024]{0:T(1024)} %get-tuple-element.312) | copy-start | bytes 12292
  728.9 50.0 %copy-start.50 = (f32[1024]{0:T(1024)S(1)}, f32[1024]{0:T(1024)}, u32[]{:S(2)}) copy-start(f32[1024]{0:T(1024)} %param.29) | copy-start | bytes 12292
  778.9 280.6 %copy-start.1 = (bf16[1024,1024]{1,0:T(8,128)(2,1)S(1)}, bf16[1024,1024]{1,0:T(8,128)(2,1)}, u32[]{:S(2)}) copy-start(bf16[1024,1024]{1,0:T(8,128)(2,1)} %param.28) | copy-start | bytes 6291460
  (32 other events, 150.8 us)
Sparse Core Ops, SparseCore 0:
  105.5 88.1 all-reduce.5
  241.6 85.6 all-reduce.7
  575.7 153.0 all-reduce.9
  732.3 75.5 reduce-scatter.4
  811.7 63.8 reduce-scatter.6
  879.6 87.6 reduce-scatter.10
  971.5 87.9 reduce-scatter.8
where the time goes:
time: 1080 us; the launch traced here: 1070 us
  waiting for transfers between devices  533 us (49%)
  matrix products  285 us (26%)
  other arithmetic  151 us (14%)
  local copies, waits for them, and re-layouts  41.2 us (4%)
  blocking collectives  38.7 us (4%)
  between operations  15.2 us (1%)
    psum x1, waiting for transfers between devices, per_device(): lax.psum(jnp.dot(activated, w_fc2, preferred_element_type=jnp.float32).as...  115 us
    reduce_scatter x1, waiting for transfers between devices, per_device(): lax.psum_scatter(grad_w_fc1, 'dp', scatter_dimension=0, tiled=True)  92.2 us
    reduce_scatter x1, waiting for transfers between devices, per_device(): lax.psum_scatter(grad_w_fc2, 'dp', scatter_dimension=1, tiled=True)  91.7 us
    psum x1, waiting for transfers between devices, per_device(): lax.psum(jnp.dot(attended, w_out, preferred_element_type=jnp.float32).ast...  88.3 us
    psum x1, waiting for transfers between devices, per_device(): lax.psum(jnp.einsum('tf,df->td', d_pre_low, w_fc1, preferred_element_type...  66.8 us
    reduce_scatter x1, waiting for transfers between devices, per_device(): lax.psum_scatter(grad_w_out, 'dp', scatter_dimension=1, tiled=True)  65.8 us
    dot_general x4, matrix products, backward_block(): jnp.einsum('qhd,khd->hqk', d_out_block, value_heads, preferred_element_ty...  45.9 us
    convert_element_type x4, other arithmetic, backward_block(): d_scores_low = d_scores.astype(jnp.bfloat16)  44.5 us
  transfers between devices with their start and end apart: 7, of which 7 were waited for; matrix products, arithmetic and copies ran while one was open for 8% of the time, Pallas kernels for 0%

commit v1 on v0

--- a/solution.py
+++ b/solution.py
@@ -2,6 +2,7 @@
 import jax.numpy as jnp
 from jax import lax
 from jax.sharding import PartitionSpec as P
+from jax.lax import all_gather
 
 HEAD = 64
 QBLOCK = 512
@@ -110,11 +111,14 @@
     grad_b_fc1 = jnp.sum(d_pre, axis=0)
     d_pre_low = d_pre.astype(jnp.bfloat16)
     grad_w_fc1 = jnp.einsum("td,tf->df", normed_two, d_pre_low, preferred_element_type=jnp.float32)
-    d_normed_two = lax.psum(
-        jnp.einsum("tf,df->td", d_pre_low, w_fc1, preferred_element_type=jnp.float32).astype(
-            jnp.bfloat16
+    d_normed_two = jnp.sum(
+        all_gather(
+            jnp.einsum("tf,df->td", d_pre_low, w_fc1, preferred_element_type=jnp.float32).astype(
+                jnp.bfloat16
+            ),
+            axis_name="mp",
         ),
-        "mp",
+        axis=0,
     ).astype(jnp.float32)
     d_middle_norm, grad_ln2_gain, grad_ln2_bias = norm_two_back(d_normed_two)
     d_middle = upstream + d_middle_norm

time: 1080 us -> 1110 us (1.028)
  waiting for transfers between devices: 533 us -> 553 us
  other arithmetic: 151 us -> 163 us
    all_gather x0 -> x1, waiting for transfers between devices: none -> 86.2 us  [per_device(): all_gather(jnp.einsum('tf,df->td', d_pre_low, w_fc1, preferred_element_ty...]
    psum x1 -> x0, waiting for transfers between devices: 66.8 us -> none  [per_device(): lax.psum(jnp.einsum('tf,df->td', d_pre_low, w_fc1, preferred_element_type...]
    reduce_sum x0 -> x1, other arithmetic: none -> 12.1 us  [per_device(): jnp.sum(all_gather(jnp.einsum('tf,df->td', d_pre_low, w_fc1, preferred_el...]
where the time goes in v1:
time: 1110 us; the launch traced here: 1100 us
  waiting for transfers between devices  553 us (50%)
  matrix products  286 us (26%)
  other arithmetic  163 us (15%)
  local copies, waits for them, and re-layouts  41.7 us (4%)
  blocking collectives  38.5 us (3%)
  between operations  15 us (1%)
    psum x1, waiting for transfers between devices, per_device(): lax.psum(jnp.dot(activated, w_fc2, preferred_element_type=jnp.float32).as...  115 us
    reduce_scatter x1, waiting for transfers between devices, per_device(): lax.psum_scatter(grad_w_fc1, 'dp', scatter_dimension=0, tiled=True)  92 us
    reduce_scatter x1, waiting for transfers between devices, per_device(): lax.psum_scatter(grad_w_fc2, 'dp', scatter_dimension=1, tiled=True)  90 us
    psum x1, waiting for transfers between devices, per_device(): lax.psum(jnp.dot(attended, w_out, preferred_element_type=jnp.float32).ast...  88.3 us
    all_gather x1, waiting for transfers between devices, per_device(): all_gather(jnp.einsum('tf,df->td', d_pre_low, w_fc1, preferred_element_ty...  86.2 us
    reduce_scatter x1, waiting for transfers between devices, per_device(): lax.psum_scatter(grad_w_out, 'dp', scatter_dimension=1, tiled=True)  68.3 us
    dot_general x4, matrix products, backward_block(): jnp.einsum('qhd,khd->hqk', d_out_block, value_heads, preferred_element_ty...  45.9 us
    convert_element_type x4, other arithmetic, backward_block(): d_scores_low = d_scores.astype(jnp.bfloat16)  44.4 us
  transfers between devices with their start and end apart: 7, of which 7 were waited for; matrix products, arithmetic and copies ran while one was open for 8% of the time, Pallas kernels for 0%

profile of v1, /device:TPU:0, one launch (start us, length us, event | category | flops | bytes accessed | tf_op | source)
XLA Modules:
  0.0 1099.3 jit_solution(10294894990419660007)
XLA Ops:
  32.3 64.2 %while.27 = (s32[]{:T(128)}, bf16[4,512,4,64]{1,3,2,0:T(8,128)(2,1)}, f32[4,4,512]{2,1,0:T(4,128)}, s32[4,512]{1,0:T(4,128)S(1)}, s32[2048]{0:T(1024)S(1)}, /*in...) while((s32[]{:T(128)}, ...), condition=%wide.region_7.8_spmd, body=%wide.region_4.7_spmd.sunk | while | flops 1125251072 | bytes 61421712 | solution.py:91
  41.8 5.9 fusion.148
  57.8 5.9 fusion.148
  73.8 5.9 fusion.148
  89.8 5.9 fusion.148
  105.3 88.3 %all-reduce.5.cloned.1.call-done = bf16[2048,1024]{1,0:T(8,128)(2,1)} async-done(((bf16[2048,1024]{1,0:T(8,128)(2,1)}), bf16[2048,1024]{1,0:T(8,128)(2,1)}) %all-reduce.5.cloned.1.call-update) | async-done | bytes 4194320 | tf_op jit(solution)/shard_map/psum | solution.py:93
  201.7 5.8 fusion.91
  207.5 25.4 %fusion.94 = (f32[1024]{0:T(1024)}, bf16[2048,1024]{1,0:T(8,128)(2,1)S(1)}, f32[2048,1024]{1,0:T(8,128)}) fusion(f32[2048,1024]{1,0:T(8,128)S(1)} %fusion.91, f32[1024]{0:T(1024)S(1)} %copy-done.53, bf16[2048,1024]{1,0:T(8,128)(2,1)S(1)} %copy-done.21, bf16[1024,1024]{1,0:T(8,128)(2,1)S(1)} %copy-done), kind=kOutput, calls=%fused_computation.147 | convolution fusion | flops 4450155520 | bytes 27271168 | tf_op jit(solution)/shard_map/td,fd->tf/dot_general | solution.py:109
  235.0 6.3 convolution_convert_fusion.1
  241.8 10.5 multiply_convert_fusion.1
  252.3 9.0 convolution_convert_fusion.2
  261.3 86.2 %all-gather.3.cloned.1.call-done = bf16[8192,1024]{1,0:T(8,128)(2,1)} async-done(((bf16[2048,1024]{1,0:T(8,128)(2,1)}), bf16[8192,1024]{1,0:T(8,128)(2,1)}) %all-gather.3.cloned.1.call-update) | async-done | bytes 16777232 | tf_op jit(solution)/shard_map/all_gather | solution.py:115
  347.5 12.1 %reduce_sum.199 = bf16[2048,1024]{1,0:T(8,128)(2,1)} reduce(bf16[4,2048,1024]{2,1,0:T(8,128)(2,1)} %bitcast.142, bf16[]{:T(256)} %constant.63.clone.1), dimensions={0}, to_apply=%region_12.13 | reduce | flops 6291456 | bytes 20971522 | tf_op jit(solution)/shard_map/reduce_sum | solution.py:114
  359.6 8.1 convert_reduce_fusion.1
  368.0 6.9 fusion.57
  374.9 6.3 fusion.96
  392.6 195.2 %while.28 = (s32[]{:T(128)}, f32[2048,4,64]{0,2,1:T(8,128)}, f32[2048,4,64]{0,2,1:T(8,128)}, f32[4,512,4,64]{1,3,2,0:T(8,128)}, bf16[4,512,4,64]{1,3,2,0:T(8,128...) while((s32[]{:T(128)}, f32[2048,4,64]{0,2,1:T(8,128)}, ...), condition=%wide.region_17.18_spmd.clone, body=%wide.region_15.17_spmd.clone.sunk | while | flops 2751068160 | bytes 164206880 | solution.py:163
  398.4 7.2 fusion.160
  405.6 11.5 %multiply_reduce_fusion.3 = (f32[4,512]{1,0:T(4,128)}, f32[4,512,2048]{2,1,0:T(8,128)}) fusion(f32[4,512,2048]{2,1,0:T(8,128)S(1)} %fusion.158, f32[4,512]{1,0:T(4,128)S(1)} %dynamic-slice_bitcast_fusion.2, pred[512,2048]{1,0:T(8,128)(4,1)} %copy-done.8, bf16[2048,4,64]{0,2,1:T(8,128)(2,1)} %get-tuple-element.520, ...), kind=kOutput, calls=%fused_computation.19.clone.1 | convolution fusion | flops 557840384 | bytes 35930116 | tf_op jit(solution)/shard_map/while/body/eval_jaxpr/qhd,khd->hqk/dot_general | solution.py:138
  417.1 11.1 %multiply_convert_fusion.3 = bf16[4,512,2048]{2,1,0:T(8,128)(2,1)} fusion(f32[4,512,2048]{2,1,0:T(8,128)} %get-tuple-element.455, f32[4,512,2048]{2,1,0:T(8,128)S(1)} %fusion.158, f32[4,512]{1,0:T(4,128)} %get-tuple-element.456, f32[4,512]{1,0:T(4,128)S(1)} %dynamic-slice_bitcast_fusion.2, pred[512,2048]{1,0:T(8,128)(4,1)} %copy-done.8), kind=kLoop, calls=%fused_computation.18.clone.1 | loop fusion | flops 25165824 | bytes 43008000 | tf_op jit(solution)/shard_map/while/body/eval_jaxpr/convert_element_type | solution.py:142
  428.2 5.3 fusion.159
  433.5 7.6 fusion.161
  446.8 7.6 fusion.160
  454.4 11.5 %multiply_reduce_fusion.3 = (f32[4,512]{1,0:T(4,128)}, f32[4,512,2048]{2,1,0:T(8,128)}) fusion(f32[4,512,2048]{2,1,0:T(8,128)S(1)} %fusion.158, f32[4,512]{1,0:T(4,128)S(1)} %dynamic-slice_bitcast_fusion.2, pred[512,2048]{1,0:T(8,128)(4,1)} %copy-done.8, bf16[2048,4,64]{0,2,1:T(8,128)(2,1)} %get-tuple-element.520, ...), kind=kOutput, calls=%fused_computation.19.clone.1 | convolution fusion | flops 557840384 | bytes 35930116 | tf_op jit(solution)/shard_map/while/body/eval_jaxpr/qhd,khd->hqk/dot_general | solution.py:138
  465.9 11.1 %multiply_convert_fusion.3 = bf16[4,512,2048]{2,1,0:T(8,128)(2,1)} fusion(f32[4,512,2048]{2,1,0:T(8,128)} %get-tuple-element.455, f32[4,512,2048]{2,1,0:T(8,128)S(1)} %fusion.158, f32[4,512]{1,0:T(4,128)} %get-tuple-element.456, f32[4,512]{1,0:T(4,128)S(1)} %dynamic-slice_bitcast_fusion.2, pred[512,2048]{1,0:T(8,128)(4,1)} %copy-done.8), kind=kLoop, calls=%fused_computation.18.clone.1 | loop fusion | flops 25165824 | bytes 43008000 | tf_op jit(solution)/shard_map/while/body/eval_jaxpr/convert_element_type | solution.py:142
  482.3 7.7 fusion.161
  495.6 7.6 fusion.160
  503.2 11.5 %multiply_reduce_fusion.3 = (f32[4,512]{1,0:T(4,128)}, f32[4,512,2048]{2,1,0:T(8,128)}) fusion(f32[4,512,2048]{2,1,0:T(8,128)S(1)} %fusion.158, f32[4,512]{1,0:T(4,128)S(1)} %dynamic-slice_bitcast_fusion.2, pred[512,2048]{1,0:T(8,128)(4,1)} %copy-done.8, bf16[2048,4,64]{0,2,1:T(8,128)(2,1)} %get-tuple-element.520, ...), kind=kOutput, calls=%fused_computation.19.clone.1 | convolution fusion | flops 557840384 | bytes 35930116 | tf_op jit(solution)/shard_map/while/body/eval_jaxpr/qhd,khd->hqk/dot_general | solution.py:138
  514.7 11.1 %multiply_convert_fusion.3 = bf16[4,512,2048]{2,1,0:T(8,128)(2,1)} fusion(f32[4,512,2048]{2,1,0:T(8,128)} %get-tuple-element.455, f32[4,512,2048]{2,1,0:T(8,128)S(1)} %fusion.158, f32[4,512]{1,0:T(4,128)} %get-tuple-element.456, f32[4,512]{1,0:T(4,128)S(1)} %dynamic-slice_bitcast_fusion.2, pred[512,2048]{1,0:T(8,128)(4,1)} %copy-done.8), kind=kLoop, calls=%fused_computation.18.clone.1 | loop fusion | flops 25165824 | bytes 43008000 | tf_op jit(solution)/shard_map/while/body/eval_jaxpr/convert_element_type | solution.py:142
  531.1 7.7 fusion.161
  544.4 7.6 fusion.160
  552.0 11.5 %multiply_reduce_fusion.3 = (f32[4,512]{1,0:T(4,128)}, f32[4,512,2048]{2,1,0:T(8,128)}) fusion(f32[4,512,2048]{2,1,0:T(8,128)S(1)} %fusion.158, f32[4,512]{1,0:T(4,128)S(1)} %dynamic-slice_bitcast_fusion.2, pred[512,2048]{1,0:T(8,128)(4,1)} %copy-done.8, bf16[2048,4,64]{0,2,1:T(8,128)(2,1)} %get-tuple-element.520, ...), kind=kOutput, calls=%fused_computation.19.clone.1 | convolution fusion | flops 557840384 | bytes 35930116 | tf_op jit(solution)/shard_map/while/body/eval_jaxpr/qhd,khd->hqk/dot_general | solution.py:138
  563.5 11.1 %multiply_convert_fusion.3 = bf16[4,512,2048]{2,1,0:T(8,128)(2,1)} fusion(f32[4,512,2048]{2,1,0:T(8,128)} %get-tuple-element.455, f32[4,512,2048]{2,1,0:T(8,128)S(1)} %fusion.158, f32[4,512]{1,0:T(4,128)} %get-tuple-element.456, f32[4,512]{1,0:T(4,128)S(1)} %dynamic-slice_bitcast_fusion.2, pred[512,2048]{1,0:T(8,128)(4,1)} %copy-done.8), kind=kLoop, calls=%fused_computation.18.clone.1 | loop fusion | flops 25165824 | bytes 43008000 | tf_op jit(solution)/shard_map/while/body/eval_jaxpr/convert_element_type | solution.py:142
  580.0 7.6 fusion.161
  599.9 7.5 bitcast_convert_fusion
  609.0 7.3 fusion.77
  616.8 10.0 fusion.100
  627.0 12.5 %fusion.74 = f32[1024,1024]{1,0:T(8,128)} fusion(bf16[2048,1024]{1,0:T(8,128)(2,1)} %copy-done.58, f32[1024]{0:T(1024)S(1)} %copy-done.57, f32[1024]{0:T(1024)S(1)} %copy-done.45, f32[2048]{0:T(1024)S(1)} %copy-done.39, bf16[2048,1024]{1,0:T(8,128)(2,1)} %all-reduce.5.cloned.1.call-done, bf16[2048,1024]{1,0:T(8,128)(2,1)} %param.19, ...), kind=kOutput, calls=%fused_computation.120 | convolution fusion | flops 4313841664 | bytes 16805888 | tf_op jit(solution)/shard_map/td,tf->df/dot_general | solution.py:113
  639.9 5.9 fusion.71
  645.9 114.6 %all-reduce.7.cloned.1.call-done = (bf16[2048,1024]{1,0:T(8,128)(2,1)}, bf16[2048,1024]{1,0:T(8,128)(2,1)}) async-done(((bf16[2048,1024]{1,0:T(8,128)(2,1)}, bf16[2048,1024]{1,0:T(8,128)(2,1)}), (bf16[2048,1024]{1,0:T(8,128)(2,1)}, bf16[2048,1024]{1,0:T(8,128)(2,1)})) %all-reduce.7.cloned.1.call-update) | async-done | bytes 8388624 | tf_op jit(solution)/shard_map/psum | solution.py:102
  760.6 5.7 convert_reduce_fusion
  766.4 5.4 fusion.58
  771.9 38.5 %all-reduce = (f32[2,256]{1,0:T(2,128)}, f32[1024]{0:T(1024)}, f32[1024]{0:T(1024)}, f32[1024]{0:T(1024)}, f32[1024]{0:T(1024)}, /*index=5*/f32[1024]{0:T(1024)}, f32[1024]{0:T(1024)}, f32[1024]{0:T(1024)}) all-reduce(f32[2,256]{1,0:T(2,128)S(1)} %pad_maximum_fusion.3, ...), channel_id=1, replica_groups=mesh['dp'=8,'mp'=4] {'dp'}, use_global_device_ids=true, to_apply=%region_24.25 | all-reduce | flops 7680 | bytes 61440 | tf_op jit(solution)/shard_map/psum | solution.py:186
  810.4 16.0 %add_add_fusion.2 = (f32[2048,1024]{1,0:T(8,128)}, bf16[2048,1024]{1,0:T(8,128)(2,1)}) fusion(f32[2048,1024]{1,0:T(8,128)} %copy-done.9, bf16[2048,1024]{1,0:T(8,128)(2,1)} %param.19, bf16[2048,1024]{1,0:T(8,128)(2,1)} %get-tuple-element.311, f32[2048]{0:T(1024)S(1)} %negate_multiply_fusion.1, f32[2048]{0:T(1024)S(1)} %multiply_multiply_fusion.5, ...), kind=kLoop, calls=%fused_computation.83 | loop fusion | flops 35651584 | bytes 37793792 | tf_op jit(solution)/shard_map/add | solution.py:179
  826.5 13.6 %reduce-scatter.5.cloned.1.call-done = f32[3,128,256]{1,2,0:T(8,128)} async-done(((f32[3,1024,256]{1,2,0:T(8,128)}), f32[3,128,256]{1,2,0:T(8,128)}) %reduce-scatter.5.cloned.1.call-update) | async-done | bytes 393232 | tf_op jit(solution)/shard_map/reduce_scatter | solution.py:181
  841.9 90.0 %reduce-scatter.11.cloned.1.call-done = f32[1024,128]{1,0:T(8,128)} async-done(((f32[1024,1024]{1,0:T(8,128)}), f32[1024,128]{1,0:T(8,128)}) %reduce-scatter.11.cloned.1.call-update) | async-done | bytes 524304 | tf_op jit(solution)/shard_map/reduce_scatter | solution.py:184
  931.9 92.0 %reduce-scatter.9.cloned.1.call-done = f32[128,1024]{1,0:T(8,128)} async-done(((f32[1024,1024]{1,0:T(8,128)}), f32[128,1024]{1,0:T(8,128)}) %reduce-scatter.9.cloned.1.call-update) | async-done | bytes 524304 | tf_op jit(solution)/shard_map/reduce_scatter | solution.py:183
  1023.9 68.3 %reduce-scatter.7.cloned.1.call-done = f32[256,128]{1,0:T(8,128)} async-done(((f32[256,1024]{1,0:T(8,128)}), f32[256,128]{1,0:T(8,128)}) %reduce-scatter.7.cloned.1.call-update) | async-done | bytes 131088 | tf_op jit(solution)/shard_map/reduce_scatter | solution.py:182
  (245 shorter events, 150.8 us)
Async XLA Ops:
  7.2 200.3 %copy-start = (bf16[1024,1024]{1,0:T(8,128)(2,1)S(1)}, bf16[1024,1024]{1,0:T(8,128)(2,1)}, u32[]{:S(2)}) copy-start(bf16[1024,1024]{1,0:T(8,128)(2,1)} %param.28) | copy-start | bytes 6291460
  7.2 9.1 copy-start.42
  7.2 9.1 copy-start.50
  7.2 186.4 %all-reduce.5.cloned.1.call-start = ((), (), s32[]{:S(2)}) async-start(), calls=%async_computation.4 | async-start | bytes 8388608 | tf_op jit(solution)/shard_map/psum | solution.py:93
  9.1 8.9 copy-start.55
  97.2 8.1 copy-start.6
  97.2 8.1 copy-start.24
  97.2 96.4 %copy-start.33 = (f32[1024]{0:T(1024)S(1)}, f32[1024]{0:T(1024)}, u32[]{:S(2)}) copy-start(f32[1024]{0:T(1024)} %param.25) | copy-start | bytes 12292
  105.3 96.4 %copy-start.44 = (f32[1024]{0:T(1024)S(1)}, f32[1024]{0:T(1024)}, u32[]{:S(2)}) copy-start(f32[1024]{0:T(1024)} %param.32) | copy-start | bytes 12292
  105.3 96.4 %copy-start.56 = (f32[1024]{0:T(1024)S(1)}, f32[1024]{0:T(1024)}, u32[]{:S(2)}) copy-start(f32[1024]{0:T(1024)} %param.33) | copy-start | bytes 12292
  105.3 242.2 %all-gather.3.cloned.1.call-start = ((), (), s32[]{:S(2)}) async-start(), calls=%async_computation.9 | async-start | bytes 20971520 | tf_op jit(solution)/shard_map/all_gather | solution.py:115
  199.5 175.4 %copy-start.31 = (f32[2048]{0:T(1024)}, f32[2048]{0:T(1024)S(1)}, u32[]{:S(2)}) copy-start(f32[2048]{0:T(1024)S(1)} %broadcast_multiply_fusion) | copy-start | bytes 24580
  201.7 173.2 %copy-start.38 = (f32[2048]{0:T(1024)}, f32[2048]{0:T(1024)S(1)}, u32[]{:S(2)}) copy-start(f32[2048]{0:T(1024)S(1)} %fusion.87) | copy-start | bytes 24580
  207.5 25.4 %copy-start.19 = (f32[2048,1024]{1,0:T(8,128)}, f32[2048,1024]{1,0:T(8,128)S(1)}, u32[]{:S(2)}) copy-start(f32[2048,1024]{1,0:T(8,128)S(1)} %fusion.91) | copy-start | bytes 25165828
  241.3 519.2 %all-reduce.7.cloned.1.call-start = ((), (), s32[]{:S(2)}) async-start(), calls=%async_computation.10 | async-start | bytes 16777216 | tf_op jit(solution)/shard_map/psum | solution.py:102
  359.6 8.1 copy-start.4
  359.6 8.1 copy-start.11
  359.6 8.3 copy-start.14
  374.9 9.8 copy-start.23
  417.1 11.1 %copy-start.12 = (f32[2048,4,64]{0,2,1:T(8,128)S(1)}, f32[2048,4,64]{0,2,1:T(8,128)}, u32[]{:S(2)}) copy-start(f32[2048,4,64]{0,2,1:T(8,128)} %get-tuple-element.498) | copy-start | bytes 6291460 | tf_op jit(solution)/shard_map/while
  428.2 13.0 %copy-start.26 = (s32[2048]{0:T(1024)S(1)}, s32[2048]{0:T(1024)}, u32[]{:S(2)}) copy-start(s32[2048]{0:T(1024)} %get-tuple-element.570) | copy-start | bytes 24580 | tf_op jit(solution)/shard_map/while
  465.9 11.1 %copy-start.12 = (f32[2048,4,64]{0,2,1:T(8,128)S(1)}, f32[2048,4,64]{0,2,1:T(8,128)}, u32[]{:S(2)}) copy-start(f32[2048,4,64]{0,2,1:T(8,128)} %get-tuple-element.498) | copy-start | bytes 6291460 | tf_op jit(solution)/shard_map/while
  477.0 13.0 %copy-start.26 = (s32[2048]{0:T(1024)S(1)}, s32[2048]{0:T(1024)}, u32[]{:S(2)}) copy-start(s32[2048]{0:T(1024)} %get-tuple-element.570) | copy-start | bytes 24580 | tf_op jit(solution)/shard_map/while
  514.7 11.1 %copy-start.12 = (f32[2048,4,64]{0,2,1:T(8,128)S(1)}, f32[2048,4,64]{0,2,1:T(8,128)}, u32[]{:S(2)}) copy-start(f32[2048,4,64]{0,2,1:T(8,128)} %get-tuple-element.498) | copy-start | bytes 6291460 | tf_op jit(solution)/shard_map/while
  525.8 13.0 %copy-start.26 = (s32[2048]{0:T(1024)S(1)}, s32[2048]{0:T(1024)}, u32[]{:S(2)}) copy-start(s32[2048]{0:T(1024)} %get-tuple-element.570) | copy-start | bytes 24580 | tf_op jit(solution)/shard_map/while
  563.5 11.1 %copy-start.12 = (f32[2048,4,64]{0,2,1:T(8,128)S(1)}, f32[2048,4,64]{0,2,1:T(8,128)}, u32[]{:S(2)}) copy-start(f32[2048,4,64]{0,2,1:T(8,128)} %get-tuple-element.498) | copy-start | bytes 6291460 | tf_op jit(solution)/shard_map/while
  574.6 13.0 %copy-start.26 = (s32[2048]{0:T(1024)S(1)}, s32[2048]{0:T(1024)}, u32[]{:S(2)}) copy-start(s32[2048]{0:T(1024)} %get-tuple-element.570) | copy-start | bytes 24580 | tf_op jit(solution)/shard_map/while
  607.5 232.6 %reduce-scatter.5.cloned.1.call-start = ((), (), s32[]{:S(2)}) async-start(), calls=%async_computation.5 | async-start | bytes 3538944 | tf_op jit(solution)/shard_map/reduce_scatter | solution.py:181
  616.3 10.6 copy-start.32
  616.3 10.6 copy-start.34
  616.3 10.6 copy-start.39
  616.4 10.6 copy-start.45
  616.4 10.6 copy-start.57
  616.4 315.5 %reduce-scatter.11.cloned.1.call-start = ((), (), s32[]{:S(2)}) async-start(), calls=%async_computation.8 | async-start | bytes 4718592 | tf_op jit(solution)/shard_map/reduce_scatter | solution.py:184
  626.9 13.0 %copy-start.18 = (bf16[32,8,4,512]{3,1,2,0:T(8,128)(2,1)S(1)}, bf16[32,8,4,512]{3,1,2,0:T(8,128)(2,1)}, u32[]{:S(2)}) copy-start(bf16[32,8,4,512]{3,1,2,0:T(8,128)(2,1)} %copy-done.17) | copy-start | bytes 3145732
  626.9 397.1 %reduce-scatter.9.cloned.1.call-start = ((), (), s32[]{:S(2)}) async-start(), calls=%async_computation.7 | async-start | bytes 4718592 | tf_op jit(solution)/shard_map/reduce_scatter | solution.py:183
  639.5 121.0 %copy-start.30 = (f32[2048]{0:T(1024)S(1)}, f32[2048]{0:T(1024)}, u32[]{:S(2)}) copy-start(f32[2048]{0:T(1024)} %copy-done.29) | copy-start | bytes 24580
  639.5 121.0 %copy-start.43 = (f32[1024]{0:T(1024)S(1)}, f32[1024]{0:T(1024)}, u32[]{:S(2)}) copy-start(f32[1024]{0:T(1024)} %param.30) | copy-start | bytes 12292
  639.5 452.7 %reduce-scatter.7.cloned.1.call-start = ((), (), s32[]{:S(2)}) async-start(), calls=%async_computation.6 | async-start | bytes 1179648 | tf_op jit(solution)/shard_map/reduce_scatter | solution.py:182
  639.9 126.4 %copy-start.41 = (f32[2048]{0:T(1024)S(1)}, f32[2048]{0:T(1024)}, u32[]{:S(2)}) copy-start(f32[2048]{0:T(1024)} %copy-done.40) | copy-start | bytes 24580
  639.9 126.4 %copy-start.36 = (f32[2048]{0:T(1024)S(1)}, f32[2048]{0:T(1024)}, u32[]{:S(2)}) copy-start(f32[2048]{0:T(1024)} %copy-done.35) | copy-start | bytes 24580
  760.5 11.3 %copy-start.46 = (f32[1024]{0:T(1024)S(1)}, f32[1024]{0:T(1024)}, u32[]{:S(2)}) copy-start(f32[1024]{0:T(1024)} %get-tuple-element.260) | copy-start | bytes 12292
  760.5 11.3 %copy-start.47 = (f32[1024]{0:T(1024)S(1)}, f32[1024]{0:T(1024)}, u32[]{:S(2)}) copy-start(f32[1024]{0:T(1024)} %get-tuple-element.256) | copy-start | bytes 12292
  760.5 11.3 %copy-start.48 = (f32[1024]{0:T(1024)S(1)}, f32[1024]{0:T(1024)}, u32[]{:S(2)}) copy-start(f32[1024]{0:T(1024)} %get-tuple-element.315) | copy-start | bytes 12292
  760.5 11.3 %copy-start.49 = (f32[1024]{0:T(1024)S(1)}, f32[1024]{0:T(1024)}, u32[]{:S(2)}) copy-start(f32[1024]{0:T(1024)} %get-tuple-element.321) | copy-start | bytes 12292
  760.6 11.3 %copy-start.52 = (f32[1024]{0:T(1024)S(1)}, f32[1024]{0:T(1024)}, u32[]{:S(2)}) copy-start(f32[1024]{0:T(1024)} %get-tuple-element.312) | copy-start | bytes 12292
  760.6 49.9 %copy-start.51 = (f32[1024]{0:T(1024)S(1)}, f32[1024]{0:T(1024)}, u32[]{:S(2)}) copy-start(f32[1024]{0:T(1024)} %param.29) | copy-start | bytes 12292
  810.4 281.8 %copy-start.1 = (bf16[1024,1024]{1,0:T(8,128)(2,1)S(1)}, bf16[1024,1024]{1,0:T(8,128)(2,1)}, u32[]{:S(2)}) copy-start(bf16[1024,1024]{1,0:T(8,128)(2,1)} %param.28) | copy-start | bytes 6291460
  (33 other events, 152.5 us)
Sparse Core Ops, SparseCore 0:
  105.4 88.1 all-reduce.4
  241.4 106.0 all-gather.2
  607.6 152.8 all-reduce.6
  764.0 75.9 reduce-scatter.4
  844.1 87.7 reduce-scatter.10
  936.0 87.9 reduce-scatter.8
  1027.9 64.2 reduce-scatter.6
